TPU v7x, 32 devices: a whole 2x2x4 slice. The times are simulated.
32 devices in a mesh: lat: 8 (over y, x, core), lon: 4 (over z).
Axes of the slice: x: 2, y: 2, z: 4, core: 2. Of those that a mesh axis runs over, the one named last changes fastest.
Arguments:
- tokens: bfloat16 [4, 64, 128, 1024], P(None, 'lat', 'lon'), may hold values from -6 to 6
- qkv_weight: bfloat16 [3072, 1024], P(('lat', 'lon')), may hold values from -0.1875 to 0.1875
- proj_weight: bfloat16 [1024, 1024], P(('lat', 'lon')), may hold values from -0.1875 to 0.1875
- up_weight: bfloat16 [4096, 1024], P(('lat', 'lon')), may hold values from -0.1875 to 0.1875
- down_weight: bfloat16 [4096, 1024], P(('lat', 'lon')), may hold values from -0.09375 to 0.09375
- bias_table: float32 [225, 16], replicated, may hold values from -3 to 220
- sea_mask: int32 [64, 128], replicated, may hold values 0 or 1
Outputs:
- block_out: bfloat16 [4, 64, 128, 1024], P(None, 'lat', 'lon')
All inputs are finite; a program needn't handle non-finite values.
Results may differ from a plain program's by a relative error of at most 0.012.
Values may be sent and summed in bfloat16 or wider, within the bound.
A program may use at most 128 MiB of HBM per device.

v0:
```python
import jax
import jax.numpy as jnp
from jax import lax
from jax.sharding import PartitionSpec as P


def from_behind(value, axis, steps):
    count = lax.axis_size(axis)
    pairs = [(source, (source + steps) % count) for source in range(count)]
    return lax.ppermute(value, axis, pairs)


def layer_norm(values):
    widened = values.astype(jnp.float32)
    centre = jnp.mean(widened, axis=-1, keepdims=True)
    spread = jnp.mean(jnp.square(widened - centre), axis=-1, keepdims=True)
    return ((widened - centre) * lax.rsqrt(spread + 1e-05)).astype(jnp.bfloat16)


def offsets_table():
    cell_ids = jnp.arange(64, dtype=jnp.int32)
    row_of = cell_ids // 8
    col_of = cell_ids % 8
    return (row_of[:, None] - row_of[None, :] + 7) * 15 + (col_of[:, None] - col_of[None, :] + 7)


def row_region(row_ids, total_rows):
    return jnp.where(row_ids < 4, 2, jnp.where(row_ids >= total_rows - 4, 1, 0)).astype(jnp.int32)


def window_attention(queries, pair_cells, row_start, col_start, sea_mask, pos_bias):
    batch_size, row_count, col_count, feat_width = queries.shape
    head_count = pos_bias.shape[0]
    head_size = feat_width // head_count
    lat_cells, lon_cells = sea_mask.shape
    down_count = row_count // 8
    across_count = col_count // 8
    window_count = down_count * across_count

    def to_windows(values):
        last_dim = values.shape[-1]
        shaped = values.reshape(batch_size, down_count, 8, across_count, 8, last_dim)
        return shaped.transpose(0, 1, 3, 2, 4, 5).reshape(batch_size, window_count, 64, last_dim)

    query_win = to_windows(queries)
    pair_win = to_windows(pair_cells)
    grid_rows = (row_start + jnp.arange(row_count, dtype=jnp.int32)) % lat_cells
    region = row_region(grid_rows, lat_cells).reshape(down_count, 8)
    region = jnp.broadcast_to(region[:, None, :, None], (down_count, across_count, 8, 8)).reshape(
        window_count, 64
    )
    sea_tiled = jnp.tile(sea_mask, (2, 2))
    sea_keep = lax.dynamic_slice(
        sea_tiled, (row_start % lat_cells, col_start % lon_cells), (row_count, col_count)
    )
    sea_keep = (
        sea_keep.reshape(down_count, 8, across_count, 8)
        .transpose(0, 2, 1, 3)
        .reshape(window_count, 64)
        == 1
    )
    same_cell = jnp.eye(64, dtype=bool)
    allowed = (region[:, :, None] == region[:, None, :]) & (sea_keep[:, None, :] | same_cell[None])
    group_width = 4 * head_size
    score_scale = head_size ** (-0.5)

    def one_group(group_index):
        first_col = group_index * group_width
        split_shape = (batch_size, window_count, 64, 4, head_size)
        query_part = lax.dynamic_slice_in_dim(query_win, first_col, group_width, 3).reshape(
            split_shape
        )
        key_part = lax.dynamic_slice_in_dim(pair_win, first_col, group_width, 3).reshape(
            split_shape
        )
        value_part = lax.dynamic_slice_in_dim(
            pair_win, feat_width + first_col, group_width, 3
        ).reshape(split_shape)
        bias_part = lax.dynamic_slice_in_dim(pos_bias, group_index * 4, 4, 0)
        scores = jnp.einsum(
            "bsqhd,bskhd->bshqk", query_part, key_part, preferred_element_type=jnp.float32
        )
        scores = scores * score_scale + bias_part[None, None]
        scores = jnp.where(allowed[None, :, None], scores, -1e30)
        row_top = jnp.max(scores, axis=-1, keepdims=True)
        weights = jnp.exp(scores - row_top)
        attn_probs = (weights / jnp.sum(weights, axis=-1, keepdims=True)).astype(jnp.bfloat16)
        context = jnp.einsum(
            "bshqk,bskhd->bsqhd", attn_probs, value_part, preferred_element_type=jnp.float32
        )
        return context.astype(jnp.bfloat16).reshape(batch_size, window_count, 64, group_width)

    groups = lax.map(one_group, jnp.arange(head_count // 4, dtype=jnp.int32))
    context = jnp.transpose(groups, (1, 2, 3, 0, 4)).reshape(
        batch_size, down_count, across_count, 8, 8, feat_width
    )
    return context.transpose(0, 1, 3, 2, 4, 5).reshape(batch_size, row_count, col_count, feat_width)


def per_device(tokens, qkv_weight, proj_weight, up_weight, down_weight, bias_table, sea_mask):
    batch_size, lat_rows, lon_cols, feat_width = tokens.shape
    head_count = bias_table.shape[1]
    row_base = lax.axis_index("lat") * lat_rows
    col_base = lax.axis_index("lon") * lon_cols
    offset_ids = offsets_table().reshape(-1)
    one_hot = (
        offset_ids[:, None] == jnp.arange(bias_table.shape[0], dtype=jnp.int32)[None, :]
    ).astype(jnp.float32)
    pos_bias = jnp.dot(one_hot, bias_table, precision=lax.Precision.HIGHEST)
    pos_bias = pos_bias.reshape(64, 64, head_count).transpose(2, 0, 1)
    normed = layer_norm(tokens)
    arrived = from_behind(normed[:, :4], "lat", -1)
    rolled_rows = jnp.concatenate([normed[:, 4:], arrived], axis=1)
    arrived_cols = from_behind(rolled_rows[:, :, :4], "lon", -1)
    feed_cells = jnp.concatenate([rolled_rows[:, :, 4:], arrived_cols], axis=2)
    feed_flat = feed_cells.reshape(-1, feat_width)
    projected = lax.dot_general(
        feed_flat,
        lax.all_gather(qkv_weight, ("lat", "lon"), axis=0, tiled=True),
        (((1,), (1,)), ((), ())),
        preferred_element_type=jnp.float32,
    ).astype(jnp.bfloat16)
    projected = projected.reshape(batch_size, lat_rows, lon_cols, 3 * feat_width)
    queries = projected[..., :feat_width]
    pair_cells = projected[..., feat_width:]
    rolled_context = window_attention(
        queries, pair_cells, row_base + 4, col_base + 4, sea_mask, pos_bias
    )
    came_cols = from_behind(rolled_context[:, :, lon_cols - 4 :], "lon", 1)
    back_cols = jnp.concatenate([came_cols, rolled_context[:, :, : lon_cols - 4]], axis=2)
    came_rows = from_behind(back_cols[:, lat_rows - 4 :], "lat", 1)
    context = jnp.concatenate([came_rows, back_cols[:, : lat_rows - 4]], axis=1)
    context_flat = context.reshape(-1, feat_width)
    attention_out = lax.dot_general(
        context_flat,
        lax.all_gather(proj_weight, ("lat", "lon"), axis=0, tiled=True),
        (((1,), (1,)), ((), ())),
        preferred_element_type=jnp.float32,
    )
    attended = (tokens.reshape(-1, feat_width).astype(jnp.float32) + attention_out).astype(
        jnp.bfloat16
    )
    normed_two = layer_norm(attended)
    up_part = lax.all_gather(up_weight, ("lat", "lon"), axis=0, tiled=True)
    down_part = lax.all_gather(down_weight, ("lat", "lon"), axis=0, tiled=True)
    hidden = lax.dot_general(
        normed_two, up_part, (((1,), (1,)), ((), ())), preferred_element_type=jnp.float32
    )
    hidden = jax.nn.gelu(hidden).astype(jnp.bfloat16)
    hidden_sum = jnp.dot(hidden, down_part, preferred_element_type=jnp.float32)
    result = (attended.astype(jnp.float32) + hidden_sum).astype(jnp.bfloat16)
    return result.reshape(tokens.shape)


def solution(mesh):
    placed = (
        P(None, "lat", "lon", None),
        P(("lat", "lon"), None),
        P(("lat", "lon"), None),
        P(("lat", "lon"), None),
        P(("lat", "lon"), None),
        P(),
        P(),
    )
    return jax.shard_map(
        per_device,
        mesh=mesh,
        in_specs=placed,
        out_specs=P(None, "lat", "lon", None),
        check_vma=False,
    )
```

profile of v0, /device:TPU:0, one launch (start us, length us, event | category | flops | bytes accessed | tf_op | source)
XLA Modules:
  0.0 342.3 jit_solution(10665718316045171469)
XLA Ops:
  6.5 0.7 all-gather.5.cloned.1.call-update
  7.3 0.7 all-gather.7.cloned.1.call-update
  8.1 0.7 all-gather.11.cloned.1.call-update
  8.8 0.5 all-gather.9.cloned.1.call-update
  9.3 1.9 convert_reduce_fusion.1
  11.3 0.7 multiply_reduce_fusion
  12.0 0.6 multiply_convert_fusion
  12.6 1.2 fusion.70
  13.7 3.4 collective-permute-start
  17.8 2.6 fusion.42
  20.6 1.0 copy.26
  21.6 9.6 %collective-permute-done = bf16[4,4,32,1024]{3,2,1,0:T(8,128)(2,1)S(1)} collective-permute-done((bf16[4,4,32,1024]{3,2,1,0:T(8,128)(2,1)}, bf16[4,4,32,1024]{3,2,1,0:T(8,128)(2,1)S(1)}, u32[]{:S(2)}, u32[]{:S(2)}) %collective-permute-start) | collective-permute-done | bytes 1048608 | tf_op jit(solution)/shard_map/ppermute | solution.py:10
  31.3 3.6 %collective-permute-start.1 = (bf16[4,8,4,1024]{3,2,1,0:T(4,128)(2,1)S(1)}, bf16[4,8,4,1024]{3,2,1,0:T(4,128)(2,1)S(1)}, u32[]{:S(2)}, u32[]{:S(2)}) collective-permute-start(bf16[4,8,4,1024]{3,2,1,0:T(4,128)(2,1)S(1)} %pad_maximum_fusion.2), channel_id=1, source_target_pairs={{0,3},{1,0},{2,1},{3,2},{4,7},{5,4},{6,5},{7,6},{8,11},{9,8},{10,9... | collective-permute-start | bytes 786440 | tf_op jit(solution)/shard_map/ppermute | solution.py:10
  34.9 0.5 slice_maximum_fusion
  35.5 5.3 %collective-permute-done.1 = bf16[4,8,4,1024]{3,2,1,0:T(4,128)(2,1)S(1)} collective-permute-done((bf16[4,8,4,1024]{3,2,1,0:T(4,128)(2,1)S(1)}, bf16[4,8,4,1024]{3,2,1,0:T(4,128)(2,1)S(1)}, u32[]{:S(2)}, u32[]{:S(2)}) %collective-permute-start.1) | collective-permute-done | bytes 262176 | tf_op jit(solution)/shard_map/ppermute | solution.py:10
  41.1 47.4 %all-gather.5.cloned.1.call-done = bf16[3072,1024]{1,0:T(8,128)(2,1)} async-done(((bf16[96,1024]{1,0:T(8,128)(2,1)}), bf16[3072,1024]{1,0:T(8,128)(2,1)}) %all-gather.5.cloned.1.call-update) | async-done | bytes 6291472 | tf_op jit(solution)/shard_map/all_gather | solution.py:119
  88.5 9.7 %convolution_convert_fusion.1 = bf16[1024,3072]{1,0:T(8,128)(2,1)S(1)} fusion(bf16[1024,1024]{1,0:T(8,128)(2,1)S(1)} %bitcast.76, bf16[3072,1024]{1,0:T(8,128)(2,1)} %all-gather.5.cloned.1.call-done), kind=kOutput, calls=%fused_computation.36 | convolution fusion | flops 6445596672 | bytes 14680064 | tf_op jit(solution)/shard_map/dot_general | solution.py:117
  98.2 1.5 copy_bitcast_fusion.2
  99.7 2.3 copy_bitcast_fusion
  102.1 45.2 %while.13 = (s32[]{:T(128)}, bf16[4,4,4,64,256]{3,4,2,1,0:T(8,128)(2,1)}, s32[4]{0:T(128)S(1)}, bf16[4,4,64,2048]{3,2,1,0:T(8,128)(2,1)}, bf16[4,4,64,1024]{3,2,...) while((s32[]{:T(128)}, ...), condition=%wide.region_5.6_spmd.clone, body=%wide.region_2.5_spmd.clone.sunk | while | flops 69255248 | bytes 12326224 | solution.py:93
  102.1 0.6 dynamic_slice.50
  103.2 1.5 constant_dynamic-slice_fusion.6
  105.1 0.4 reshape.231
  106.1 0.9 constant_dynamic-slice_fusion.7
  107.2 2.6 fusion.87
  109.8 0.5 copy.62
  110.3 2.0 convolution_convert_fusion.3
  112.3 1.1 constant_dynamic-update-slice_fusion.2
  113.4 0.6 dynamic_slice.50
  114.5 1.5 constant_dynamic-slice_fusion.6
  116.4 0.4 reshape.231
  117.4 0.9 constant_dynamic-slice_fusion.7
  118.4 2.6 fusion.87
  121.0 0.5 copy.62
  121.5 2.0 convolution_convert_fusion.3
  123.6 1.1 constant_dynamic-update-slice_fusion.2
  124.7 0.6 dynamic_slice.50
  125.8 1.5 constant_dynamic-slice_fusion.6
  127.3 0.4 reshape.230
  128.7 0.9 constant_dynamic-slice_fusion.7
  129.7 2.6 fusion.87
  132.3 0.5 copy.62
  132.8 2.0 convolution_convert_fusion.3
  134.8 1.1 constant_dynamic-update-slice_fusion.2
  136.0 0.6 dynamic_slice.50
  137.1 1.5 constant_dynamic-slice_fusion.6
  140.0 0.9 constant_dynamic-slice_fusion.7
  141.1 2.6 fusion.87
  143.7 0.5 copy.62
  144.2 2.0 convolution_convert_fusion.3
  146.2 1.0 constant_dynamic-update-slice_fusion.2
  147.2 5.5 %copy.28 = bf16[4,4,64,4,256]{4,3,2,1,0:T(4,128)(2,1)S(1)} copy(bf16[4,4,64,4,256]{2,4,1,0,3:T(8,128)(2,1)} %bitcast.11) | data formatting | bytes 4194304 | tf_op jit(solution)/shard_map/transpose | solution.py:94
  152.8 2.7 reshape.220
  155.5 1.9 copy_bitcast_fusion.1
  157.5 1.8 collective-permute-start.2
  159.3 13.3 %collective-permute-done.2 = bf16[4,8,4,1024]{3,2,1,0:T(4,128)(2,1)S(1)} collective-permute-done((bf16[4,8,4,1024]{3,2,1,0:T(4,128)(2,1)S(1)}, bf16[4,8,4,1024]{3,2,1,0:T(4,128)(2,1)S(1)}, u32[]{:S(2)}, u32[]{:S(2)}) %collective-permute-start.2) | collective-permute-done | bytes 262176 | tf_op jit(solution)/shard_map/ppermute | solution.py:10
  173.1 22.6 %collective-permute-done.3 = bf16[4,4,32,1024]{3,2,1,0:T(8,128)(2,1)S(1)} collective-permute-done((bf16[4,4,32,1024]{3,2,1,0:T(8,128)(2,1)S(1)}, bf16[4,4,32,1024]{3,2,1,0:T(8,128)(2,1)S(1)}, u32[]{:S(2)}, u32[]{:S(2)}) %collective-permute-start.3) | collective-permute-done | bytes 1048608 | tf_op jit(solution)/shard_map/ppermute | solution.py:10
  195.7 1.8 fusion.49
  197.5 4.7 %convert_reduce_fusion = (f32[1024]{0:T(1024)S(1)}, bf16[1024,1024]{1,0:T(8,128)(2,1)S(1)}) fusion(bf16[1024,1024]{1,0:T(8,128)(2,1)} %bitcast.75, bf16[1024,1024]{1,0:T(8,128)(2,1)} %all-gather.7.cloned.1.call-done, bf16[4,8,32,1024]{3,2,1,0:T(8,128)(2,1)S(1)} %copy-done.3), kind=kOutput, calls=%fused_computation.35 | convolution fusion | flops 2152725504 | bytes 8392704 | tf_op jit(solution)/shard_map/dot_general | solution.py:134
  202.2 1.3 copy-done.4
  203.5 0.7 fusion.38
  204.2 26.9 %all-gather.11.cloned.1.call-done = bf16[4096,1024]{1,0:T(8,128)(2,1)} async-done(((bf16[128,1024]{1,0:T(8,128)(2,1)}), bf16[4096,1024]{1,0:T(8,128)(2,1)}) %all-gather.11.cloned.1.call-update) | async-done | bytes 8388624 | tf_op jit(solution)/shard_map/all_gather | solution.py:145
  231.2 78.5 %all-gather.9.cloned.1.call-done = bf16[4096,1024]{1,0:T(8,128)(2,1)} async-done(((bf16[128,1024]{1,0:T(8,128)(2,1)}), bf16[4096,1024]{1,0:T(8,128)(2,1)}) %all-gather.9.cloned.1.call-update) | async-done | bytes 8388624 | tf_op jit(solution)/shard_map/all_gather | solution.py:144
  309.7 26.1 %fusion.40 = bf16[1024,1024]{1,0:T(8,128)(2,1)} fusion(bf16[1024,1024]{1,0:T(8,128)(2,1)} %copy-done.4, bf16[4096,1024]{1,0:T(8,128)(2,1)} %all-gather.11.cloned.1.call-done, bf16[4096,1024]{1,0:T(8,128)(2,1)} %all-gather.9.cloned.1.call-done, f32[1024]{0:T(1024)S(1)} %add_rsqrt_fusion.1, f32[1024]{0:T(1024)S(1)} %broadcast_multiply_fusion.1), kind=kOutput, calls=%fused_computation.41 | convolution fusion | flops 17224957952 | bytes 20979712 | tf_op jit(solution)/shard_map/dot_general | solution.py:150
  (50 shorter events, 4.6 us)
Async XLA Ops:
  6.5 11.3 %copy-start = (f32[225,16]{0,1:T(8,128)S(1)}, f32[225,16]{0,1:T(8,128)}, u32[]{:S(2)}) copy-start(f32[225,16]{0,1:T(8,128)} %param.14) | copy-start | bytes 43204
  6.5 4.7 %copy-start.2 = (bf16[4,8,32,1024]{3,2,1,0:T(8,128)(2,1)S(1)}, bf16[4,8,32,1024]{3,2,1,0:T(8,128)(2,1)}, u32[]{:S(2)}) copy-start(bf16[4,8,32,1024]{3,2,1,0:T(8,128)(2,1)} %param.9) | copy-start | bytes 6291460
  6.5 82.0 %all-gather.5.cloned.1.call-start = ((), (), s32[]{:S(2)}) async-start(), calls=%async_computation | async-start | bytes 6488064 | tf_op jit(solution)/shard_map/all_gather | solution.py:119
  7.3 190.2 %all-gather.7.cloned.1.call-start = ((), (), s32[]{:S(2)}) async-start(), calls=%async_computation.1 | async-start | bytes 2162688 | tf_op jit(solution)/shard_map/all_gather | solution.py:136
  8.0 223.2 %all-gather.11.cloned.1.call-start = ((), (), s32[]{:S(2)}) async-start(), calls=%async_computation.3 | async-start | bytes 8650752 | tf_op jit(solution)/shard_map/all_gather | solution.py:145
  8.7 300.9 %all-gather.9.cloned.1.call-start = ((), (), s32[]{:S(2)}) async-start(), calls=%async_computation.2 | async-start | bytes 8650752 | tf_op jit(solution)/shard_map/all_gather | solution.py:144
  12.0 5.1 %copy-start.5 = (s32[64,128]{1,0:T(8,128)S(1)}, s32[64,128]{1,0:T(8,128)}, u32[]{:S(2)}) copy-start(s32[64,128]{1,0:T(8,128)} %param.15) | copy-start | bytes 98308
  13.7 17.4 %collective-permute-start = (bf16[4,4,32,1024]{3,2,1,0:T(8,128)(2,1)}, bf16[4,4,32,1024]{3,2,1,0:T(8,128)(2,1)S(1)}, u32[]{:S(2)}, u32[]{:S(2)}) collective-permute-start(bf16[4,4,32,1024]{3,2,1,0:T(8,128)(2,1)} %get-tuple-element.142), channel_id=1, source_target_pairs={{0,28},{4,0},{8,4},{12,8},{16,12},{20,16},{24,20},{28,24},{1,29},{... | collective-permute-start | bytes 3145736 | tf_op jit(solution)/shard_map/ppermute | solution.py:10
  31.3 9.5 %collective-permute-start.1 = (bf16[4,8,4,1024]{3,2,1,0:T(4,128)(2,1)S(1)}, bf16[4,8,4,1024]{3,2,1,0:T(4,128)(2,1)S(1)}, u32[]{:S(2)}, u32[]{:S(2)}) collective-permute-start(bf16[4,8,4,1024]{3,2,1,0:T(4,128)(2,1)S(1)} %pad_maximum_fusion.2), channel_id=1, source_target_pairs={{0,3},{1,0},{2,1},{3,2},{4,7},{5,4},{6,5},{7,6},{8,11},{9,8},{10,9... | collective-permute-start | bytes 786440 | tf_op jit(solution)/shard_map/ppermute | solution.py:10
  157.5 15.1 %collective-permute-start.2 = (bf16[4,8,4,1024]{3,2,1,0:T(4,128)(2,1)S(1)}, bf16[4,8,4,1024]{3,2,1,0:T(4,128)(2,1)S(1)}, u32[]{:S(2)}, u32[]{:S(2)}) collective-permute-start(bf16[4,8,4,1024]{3,2,1,0:T(4,128)(2,1)S(1)} %slice.46), channel_id=1, source_target_pairs={{0,1},{1,2},{2,3},{3,0},{4,5},{5,6},{6,7},{7,4},{8,9},{9,10},{10,1... | collective-permute-start | bytes 786440 | tf_op jit(solution)/shard_map/ppermute | solution.py:10
  172.7 24.8 %copy-start.3 = (bf16[4,8,32,1024]{3,2,1,0:T(8,128)(2,1)S(1)}, bf16[4,8,32,1024]{3,2,1,0:T(8,128)(2,1)}, u32[]{:S(2)}) copy-start(bf16[4,8,32,1024]{3,2,1,0:T(8,128)(2,1)} %param.9) | copy-start | bytes 6291460
  173.1 22.6 %collective-permute-start.3 = (bf16[4,4,32,1024]{3,2,1,0:T(8,128)(2,1)S(1)}, bf16[4,4,32,1024]{3,2,1,0:T(8,128)(2,1)S(1)}, u32[]{:S(2)}, u32[]{:S(2)}) collective-permute-start(bf16[4,4,32,1024]{3,2,1,0:T(8,128)(2,1)S(1)} %fusion.59), channel_id=1, source_target_pairs={{0,4},{4,8},{8,12},{12,16},{16,20},{20,24},{24,28},{28,0},{1,5},{5... | collective-permute-start | bytes 3145736 | tf_op jit(solution)/shard_map/ppermute | solution.py:10
  202.2 1.3 copy-start.4
  309.7 26.1 %copy-start.1 = (f32[225,16]{0,1:T(8,128)S(1)}, f32[225,16]{0,1:T(8,128)}, u32[]{:S(2)}) copy-start(f32[225,16]{0,1:T(8,128)} %param.14) | copy-start | bytes 43204
Sparse Core Ops, SparseCore 0:
  10.2 78.2 all-gather.4
  91.4 54.8 all-gather.6
  149.3 81.8 all-gather.10
  234.0 75.6 all-gather.8
where the time goes:
time: 343 us; the launch traced here: 342 us
  waiting for transfers between devices  206 us (60%)
  matrix products  61.5 us (18%)
  local copies, waits for them, and re-layouts  39.7 us (12%)
  between operations  13.3 us (4%)
  starting transfers between devices  8.92 us (3%)
  other arithmetic  7.73 us (2%)
  loops' own time  4.85 us (1%)
    all_gather x1, waiting for transfers between devices, per_device(): up_part = lax.all_gather(up_weight, ('lat', 'lon'), axis=0, tiled=True)  78.5 us
    ppermute x4, waiting for transfers between devices, from_behind(): return lax.ppermute(value, axis, pairs)  50.8 us
    all_gather x1, waiting for transfers between devices, per_device(): lax.all_gather(qkv_weight, ('lat', 'lon'), axis=0, tiled=True)  47.4 us
    all_gather x1, waiting for transfers between devices, per_device(): down_part = lax.all_gather(down_weight, ('lat', 'lon'), axis=0, tiled=True)  26.9 us
    dot_general x1, matrix products, per_device(): hidden_sum = jnp.dot(hidden, down_part, preferred_element_type=jnp.float32)  26.1 us
    sub x4, matrix products, one_group(): weights = jnp.exp(scores - row_top)  10.4 us
    dot_general x1, matrix products, per_device(): lax.dot_general(feed_flat, lax.all_gather(qkv_weight, ('lat', 'lon'), axi...  9.71 us
    ppermute x4, starting transfers between devices, from_behind(): return lax.ppermute(value, axis, pairs)  8.81 us
  transfers between devices with their start and end apart: 8, of which 7 were waited for; matrix products, arithmetic and copies ran while one was open for 24% of the time, Pallas kernels for 0%

commit v1 on v0

--- a/solution.py
+++ b/solution.py
@@ -1,7 +1,219 @@
 import jax
 import jax.numpy as jnp
 from jax import lax
+from jax.experimental import pallas as pl
+from jax.experimental.pallas import tpu as pltpu
 from jax.sharding import PartitionSpec as P
+
+
+MESH_ID = pl.DeviceIdType.MESH
+
+
+def piece_rows(rows, flip):
+    unit = 16 if rows % 16 == 0 else 8
+    units = rows // unit
+    last = (units * 3 + 6) // 13
+    first = (units - last + 1) // 2
+    second = units - last - first
+    if flip:
+        first, second = second, first
+    bounds = [0, first * unit, (first + second) * unit, rows]
+    return [(bounds[i], bounds[i + 1] - bounds[i]) for i in range(3)]
+
+
+def split_lat(lat_size):
+    inner = lat_size // 4
+    return (2, inner) if lat_size % 4 == 0 else (1, lat_size // 2)
+
+
+class Gather:
+    def __init__(self, sizes, ins, outs, stage, send_sem, recv_sem, load_sem, order):
+        self.sizes = sizes
+        self.ins, self.outs, self.stage = ins, outs, stage
+        self.send_sem, self.recv_sem, self.load_sem = send_sem, recv_sem, load_sem
+        lat, lon = lax.axis_index("lat"), lax.axis_index("lon")
+        self.core = lax.rem(lat, 2)
+        chip = lax.div(lat, 2)
+        self.at = {"y": lax.div(chip, sizes["x"]), "x": lax.rem(chip, sizes["x"]), "z": lon}
+        self.next_sem = 0
+        self.sends = []
+        self.flows = []
+        for turn, (index, offset) in enumerate(order):
+            pieces = piece_rows(ins[index].shape[0], turn % 2 == 1)
+            for axes, (start, length) in zip(("zyx", "zxy", None), pieces):
+                if length == 0:
+                    continue
+                if axes is None:
+                    axes = "xyz" if turn % 2 == 0 else "yxz"
+                self.flows.append((offset, self.steps(index, axes, start, length)))
+        self.length = max(offset + len(steps) for offset, steps in self.flows)
+
+    def device(self, axis=None, move=0):
+        place = dict(self.at)
+        core = self.core
+        if axis == "core":
+            core = 1 - core
+        elif axis is not None:
+            place[axis] = place[axis] + move
+        return ((place["y"] * self.sizes["x"] + place["x"]) * 2 + core, place["z"])
+
+    def barrier(self):
+        sem = pltpu.get_barrier_semaphore()
+        count = 0
+        for axis in "yxz":
+            size = self.sizes[axis]
+            if size == 1:
+                continue
+            for move in (1, size - 1):
+                place = dict(self.at)
+                place[axis] = lax.rem(place[axis] + move, size)
+                where = (
+                    (place["y"] * self.sizes["x"] + place["x"]) * 2 + self.core,
+                    place["z"],
+                )
+                pl.semaphore_signal(sem, inc=1, device_id=where, device_id_type=MESH_ID)
+                count += 1
+        pl.semaphore_signal(
+            sem, inc=1, device_id=self.device("core"), device_id_type=MESH_ID
+        )
+        pl.semaphore_wait(sem, count + 1)
+
+    def load(self):
+        loads = []
+        for index, ref in enumerate(self.ins):
+            copy = pltpu.make_async_copy(ref, self.stage[index], self.load_sem.at[index])
+            copy.start()
+            loads.append(copy)
+        stores = []
+        for index, copy in enumerate(loads):
+            copy.wait()
+            store = pltpu.make_async_copy(
+                self.stage[index],
+                self.outs[index].at[self.at["y"], self.at["x"], self.core, self.at["z"]],
+                self.load_sem.at[index],
+            )
+            store.start()
+            stores.append(store)
+        for store in stores:
+            store.wait()
+
+    def region(self, index, done, axis, place, start, length):
+        pick = {
+            name: (pl.ds(0, self.sizes[name]) if name in done else self.at[name]) for name in "yxz"
+        }
+        if axis is not None:
+            pick[axis] = place
+        return self.outs[index].at[
+            pick["y"], pick["x"], self.core, pick["z"], pl.ds(start, length)
+        ]
+
+    def copy(self, ref, where):
+        slot = self.next_sem
+        self.next_sem += 1
+        return pltpu.make_async_remote_copy(
+            src_ref=ref,
+            dst_ref=ref,
+            send_sem=self.send_sem.at[slot],
+            recv_sem=self.recv_sem.at[slot],
+            device_id=where,
+            device_id_type=MESH_ID,
+        )
+
+    def steps(self, index, axes, start, length):
+        steps = []
+        pending = []
+        for position, axis in enumerate(axes):
+            size = self.sizes[axis]
+            here = self.at[axis]
+            done = axes[:position]
+            for hop in range(1, size):
+                sends, waits = [], []
+                for move in (1, -1):
+                    carried = here - move * (hop - 1)
+                    can_send = (carried >= 0) & (carried < size)
+                    can_send &= (here + move >= 0) & (here + move < size)
+                    coming = here - move * hop
+                    can_get = (coming >= 0) & (coming < size)
+                    slot_ref = lambda place: self.region(index, done, axis, place, start, length)
+                    safe = jnp.clip(carried, 0, size - 1)
+                    other = jnp.clip(here + move, 0, size - 1) - here
+                    copy = self.copy(slot_ref(safe), self.device(axis, other))
+                    sends.append((can_send, copy))
+                    waits.append((can_get, copy))
+                steps.append((pending, sends))
+                self.sends += sends
+                pending = waits
+        everything = self.region(index, axes, None, None, start, length)
+        copy = self.copy(everything, self.device("core"))
+        steps.append((pending, [(None, copy)]))
+        self.sends.append((None, copy))
+        steps.append(([(None, copy)], []))
+        return steps
+
+    def tick(self, time):
+        for offset, steps in self.flows:
+            step = time - offset
+            if 0 <= step < len(steps):
+                waits, sends = steps[step]
+                for when, copy in waits:
+                    run_if(when, copy.wait_recv)
+                for when, copy in sends:
+                    run_if(when, copy.start)
+
+    def finish(self):
+        for when, copy in self.sends:
+            run_if(when, copy.wait_send)
+
+
+def run_if(when, action):
+    if when is None:
+        action()
+    else:
+        pl.when(when)(lambda: action())
+
+
+def count_copies(sizes, rows):
+    hops = sum(2 * (sizes[axis] - 1) for axis in "yxz") + 1
+    return sum(hops for count in rows for start, length in piece_rows(count, False) if length)
+
+
+def gather_weights(mesh_shape, weights, order):
+    outer, inner = split_lat(mesh_shape["lat"])
+    sizes = {"y": outer, "x": inner, "z": mesh_shape["lon"]}
+    total = len(weights)
+    copies = count_copies(sizes, [weight.shape[0] for weight in weights])
+
+    def kernel(*refs):
+        ins, outs, scratch = refs[:total], refs[total : 2 * total], refs[2 * total :]
+        stage = scratch[:total]
+        send_sem, recv_sem, load_sem = scratch[total:]
+        gather = Gather(sizes, ins, outs, stage, send_sem, recv_sem, load_sem, order)
+        gather.load()
+        gather.barrier()
+        for time in range(gather.length):
+            gather.tick(time)
+        gather.finish()
+
+    lead = (outer, inner, 2, mesh_shape["lon"])
+    outs = pl.pallas_call(
+        kernel,
+        out_shape=[
+            jax.ShapeDtypeStruct(lead + weight.shape, weight.dtype) for weight in weights
+        ],
+        in_specs=[pl.BlockSpec(memory_space=pl.ANY)] * total,
+        out_specs=[pl.BlockSpec(memory_space=pl.ANY)] * total,
+        scratch_shapes=[pltpu.VMEM(weight.shape, weight.dtype) for weight in weights]
+        + [
+            pltpu.SemaphoreType.DMA((copies,)),
+            pltpu.SemaphoreType.DMA((copies,)),
+            pltpu.SemaphoreType.DMA((total,)),
+        ],
+        compiler_params=pltpu.CompilerParams(collective_id=0, has_side_effects=True),
+        cost_estimate=pl.CostEstimate(
+            flops=90_000_000_000, bytes_accessed=50_000_000, transcendentals=0
+        ),
+    )(*weights)
+    return [out.reshape(-1, out.shape[-1]) for out in outs]
 
 
 def from_behind(value, axis, steps):
@@ -99,6 +311,12 @@
 
 def per_device(tokens, qkv_weight, proj_weight, up_weight, down_weight, bias_table, sea_mask):
     batch_size, lat_rows, lon_cols, feat_width = tokens.shape
+    mesh_shape = {"lat": lax.axis_size("lat"), "lon": lax.axis_size("lon")}
+    qkv_full, proj_full, up_full, down_full = gather_weights(
+        mesh_shape,
+        (qkv_weight, proj_weight, up_weight, down_weight),
+        ((0, 0), (1, 1), (2, 2), (3, 4)),
+    )
     head_count = bias_table.shape[1]
     row_base = lax.axis_index("lat") * lat_rows
     col_base = lax.axis_index("lon") * lon_cols
@@ -116,7 +334,7 @@
     feed_flat = feed_cells.reshape(-1, feat_width)
     projected = lax.dot_general(
         feed_flat,
-        lax.all_gather(qkv_weight, ("lat", "lon"), axis=0, tiled=True),
+        qkv_full,
         (((1,), (1,)), ((), ())),
         preferred_element_type=jnp.float32,
     ).astype(jnp.bfloat16)
@@ -133,7 +351,7 @@
     context_flat = context.reshape(-1, feat_width)
     attention_out = lax.dot_general(
         context_flat,
-        lax.all_gather(proj_weight, ("lat", "lon"), axis=0, tiled=True),
+        proj_full,
         (((1,), (1,)), ((), ())),
         preferred_element_type=jnp.float32,
     )
@@ -141,13 +359,11 @@
         jnp.bfloat16
     )
     normed_two = layer_norm(attended)
-    up_part = lax.all_gather(up_weight, ("lat", "lon"), axis=0, tiled=True)
-    down_part = lax.all_gather(down_weight, ("lat", "lon"), axis=0, tiled=True)
     hidden = lax.dot_general(
-        normed_two, up_part, (((1,), (1,)), ((), ())), preferred_element_type=jnp.float32
+        normed_two, up_full, (((1,), (1,)), ((), ())), preferred_element_type=jnp.float32
     )
     hidden = jax.nn.gelu(hidden).astype(jnp.bfloat16)
-    hidden_sum = jnp.dot(hidden, down_part, preferred_element_type=jnp.float32)
+    hidden_sum = jnp.dot(hidden, down_full, preferred_element_type=jnp.float32)
     result = (attended.astype(jnp.float32) + hidden_sum).astype(jnp.bfloat16)
     return result.reshape(tokens.shape)
 

time: 343 us -> 269 us (0.78)
  waiting for transfers between devices: 206 us -> 31.1 us
  Pallas kernels: 0 us -> 120 us
  between operations: 13.3 us -> 0.29 us
    all_gather x4 -> x0, waiting for transfers between devices: 153 us -> none  [the longest x1 78.5 us: per_device(): up_part = lax.all_gather(up_weight, ('lat', 'lon'), axis=0, tiled=True)]
    pallas_call x0 -> x1, Pallas kernels: none -> 120 us  [gather_weights(): pl.pallas_call(kernel, out_shape=[jax.ShapeDtypeStruct(lead + weight.shap...]
    ppermute x4, waiting for transfers between devices: 50.8 us -> 31.1 us  [from_behind(): return lax.ppermute(value, axis, pairs)]
  transfers between devices with their start and end apart: 8 -> 4, of which waited for: 7 -> 3; matrix products, arithmetic and copies ran while one was open for 24% -> 2% of each run, Pallas kernels for 0% -> 45%
where the time goes in v1:
time: 269 us
  Pallas kernels  120 us (45%)
  matrix products  58.8 us (22%)
  local copies, waits for them, and re-layouts  38.5 us (14%)
  waiting for transfers between devices  31.1 us (12%)
  other arithmetic  8.17 us (3%)
  starting transfers between devices  6.46 us (2%)
  loops' own time  5.18 us (2%)
    pallas_call x1, Pallas kernels, gather_weights(): pl.pallas_call(kernel, out_shape=[jax.ShapeDtypeStruct(lead + weight.shap...  120 us
    ppermute x4, waiting for transfers between devices, from_behind(): return lax.ppermute(value, axis, pairs)  31.1 us
    dot_general x1, matrix products, per_device(): hidden_sum = jnp.dot(hidden, down_full, preferred_element_type=jnp.float32)  25.5 us
    sub x4, matrix products, one_group(): weights = jnp.exp(scores - row_top)  10.4 us
    dot_general x1, matrix products, per_device(): lax.dot_general(feed_flat, qkv_full, (((1,), (1,)), ((), ())), preferred_...  9.83 us
    dot_general x4, matrix products, one_group(): jnp.einsum('bshqk,bskhd->bsqhd', attn_probs, value_part, preferred_elemen...  8.08 us
    ppermute x4, starting transfers between devices, from_behind(): return lax.ppermute(value, axis, pairs)  6.46 us
    dynamic_slice x4, local copies, waits for them, and re-layouts, one_group(): lax.dynamic_slice_in_dim(pair_win, first_col, group_width, 3)  5.94 us
  transfers between devices with their start and end apart: 4, of which 3 were waited for; matrix products, arithmetic and copies ran while one was open for 2% of the time, Pallas kernels for 45%

profile of v1, /device:TPU:0, one launch (start us, length us, event | category | flops | bytes accessed | tf_op | source)
XLA Modules:
  0.0 268.6 jit_solution(8824690488657128412)
XLA Ops:
  0.0 2.1 convert_reduce_fusion.1
  2.1 2.3 multiply_reduce_fusion
  4.4 0.5 multiply_convert_fusion
  5.0 1.2 fusion.70
  6.2 3.4 %collective-permute-start = (bf16[4,4,32,1024]{3,2,1,0:T(8,128)(2,1)}, bf16[4,4,32,1024]{3,2,1,0:T(8,128)(2,1)S(1)}, u32[]{:S(2)}, u32[]{:S(2)}) collective-permute-start(bf16[4,4,32,1024]{3,2,1,0:T(8,128)(2,1)} %get-tuple-element.150), channel_id=1, source_target_pairs={{0,28},{4,0},{8,4},{12,8},{16,12},{20,16},{24,20},{28,24},{1,29},{... | collective-permute-start | bytes 3145736 | tf_op jit(solution)/shard_map/ppermute | solution.py:222
  9.5 120.1 %shard_map.73 = (bf16[2,2,2,4,96,1024]{5,4,3,2,1,0:T(8,128)(2,1)}, bf16[2,2,2,4,32,1024]{5,4,3,2,1,0:T(8,128)(2,1)}, bf16[2,2,2,4,128,1024]{5,4,3,2,1,0:T(8,128)(2,1)}, bf16[2,2,2,4,128,1024]{5,4,3,2,1,0:T(8,128)(2,1)}) custom-call(bf16[96,1024]{1,0:T(8,128)(2,1)} %refs_0_.1, bf16[32,1024]{1,0:T(8,128)(2,1)} %refs_1_.1, bf16[128,1024]{1,0:T(8,128)(2,1)} %refs_2_.1, ...), custom_call_target="tpu_custom_call" | custom-call | flops 89999998976 | bytes 50000000 | tf_op jit(solution)/shard_map/pallas_call | solution.py:198
  130.4 2.6 fusion.42
  133.0 0.2 reshape.232
  133.2 1.0 copy.26
  134.3 2.8 %collective-permute-start.1 = (bf16[4,8,4,1024]{3,2,1,0:T(4,128)(2,1)S(1)}, bf16[4,8,4,1024]{3,2,1,0:T(4,128)(2,1)S(1)}, u32[]{:S(2)}, u32[]{:S(2)}) collective-permute-start(bf16[4,8,4,1024]{3,2,1,0:T(4,128)(2,1)S(1)} %pad_maximum_fusion.2), channel_id=1, source_target_pairs={{0,3},{1,0},{2,1},{3,2},{4,7},{5,4},{6,5},{7,6},{8,11},{9,8},{10,9... | collective-permute-start | bytes 786440 | tf_op jit(solution)/shard_map/ppermute | solution.py:222
  137.1 0.5 slice_maximum_fusion
  137.7 5.6 %collective-permute-done.1 = bf16[4,8,4,1024]{3,2,1,0:T(4,128)(2,1)S(1)} collective-permute-done((bf16[4,8,4,1024]{3,2,1,0:T(4,128)(2,1)S(1)}, bf16[4,8,4,1024]{3,2,1,0:T(4,128)(2,1)S(1)}, u32[]{:S(2)}, u32[]{:S(2)}) %collective-permute-start.1) | collective-permute-done | bytes 262176 | tf_op jit(solution)/shard_map/ppermute | solution.py:222
  143.3 0.4 pad_maximum_fusion.1
  143.7 9.8 %convolution_convert_fusion.1 = bf16[1024,3072]{1,0:T(8,128)(2,1)S(1)} fusion(bf16[1024,1024]{1,0:T(8,128)(2,1)S(1)} %bitcast.80, bf16[3072,1024]{1,0:T(8,128)(2,1)} %bitcast.86), kind=kOutput, calls=%fused_computation.36 | convolution fusion | flops 6445596672 | bytes 14680064 | tf_op jit(solution)/shard_map/dot_general | solution.py:335
  153.6 2.3 copy_bitcast_fusion
  155.9 1.5 copy_bitcast_fusion.2
  157.4 45.7 %while.13 = (s32[]{:T(128)}, bf16[4,4,4,64,256]{3,4,2,1,0:T(8,128)(2,1)}, s32[4]{0:T(128)S(1)}, bf16[4,4,64,2048]{3,2,1,0:T(8,128)(2,1)}, bf16[4,4,64,1024]{3,2,...) while((s32[]{:T(128)}, ...), condition=%wide.region_5.6_spmd.clone, body=%wide.region_2.5_spmd.clone.sunk | while | flops 69255248 | bytes 12326224 | solution.py:305
  157.4 0.6 dynamic_slice.50
  158.7 1.5 constant_dynamic-slice_fusion.6
  160.2 0.4 reshape.246
  160.6 0.4 reshape.247
  161.6 0.9 constant_dynamic-slice_fusion.7
  162.7 2.6 fusion.87
  165.2 0.5 copy.62
  165.7 2.0 convolution_convert_fusion.3
  167.8 1.1 constant_dynamic-update-slice_fusion.2
  168.8 0.6 dynamic_slice.50
  170.1 1.5 constant_dynamic-slice_fusion.6
  171.6 0.4 reshape.246
  172.0 0.4 reshape.247
  173.0 0.9 constant_dynamic-slice_fusion.7
  174.1 2.6 fusion.87
  176.7 0.5 copy.62
  177.1 2.0 convolution_convert_fusion.3
  179.2 1.1 constant_dynamic-update-slice_fusion.2
  180.2 0.6 dynamic_slice.50
  181.5 1.5 constant_dynamic-slice_fusion.6
  183.0 0.4 reshape.246
  183.4 0.4 reshape.247
  184.4 0.9 constant_dynamic-slice_fusion.7
  185.5 2.6 fusion.87
  188.1 0.5 copy.62
  188.5 2.0 convolution_convert_fusion.3
  190.6 1.1 constant_dynamic-update-slice_fusion.2
  191.7 0.6 dynamic_slice.50
  193.0 1.5 constant_dynamic-slice_fusion.6
  194.5 0.4 reshape.246
  194.9 0.4 reshape.247
  195.9 0.9 constant_dynamic-slice_fusion.7
  196.9 2.6 fusion.87
  199.5 0.5 copy.62
  200.0 2.0 convolution_convert_fusion.3
  202.1 1.1 constant_dynamic-update-slice_fusion.2
  203.1 5.5 %copy.28 = bf16[4,4,64,4,256]{4,3,2,1,0:T(4,128)(2,1)S(1)} copy(bf16[4,4,64,4,256]{2,4,1,0,3:T(8,128)(2,1)} %bitcast.12) | data formatting | bytes 4194304 | tf_op jit(solution)/shard_map/transpose | solution.py:306
  208.6 2.7 %reshape.233 = bf16[4,1,4,8,8,1024]{5,4,3,2,0,1:T(8,128)(2,1)} reshape(bf16[4,4,64,4,256]{4,3,2,1,0:T(4,128)(2,1)S(1)} %copy.28) | data formatting | bytes 4194304 | tf_op jit(solution)/shard_map/reshape | solution.py:306
  211.3 1.8 copy_bitcast_fusion.1
  213.4 10.4 %collective-permute-done.2 = bf16[4,8,4,1024]{3,2,1,0:T(4,128)(2,1)S(1)} collective-permute-done((bf16[4,8,4,1024]{3,2,1,0:T(4,128)(2,1)S(1)}, bf16[4,8,4,1024]{3,2,1,0:T(4,128)(2,1)S(1)}, u32[]{:S(2)}, u32[]{:S(2)}) %collective-permute-start.2) | collective-permute-done | bytes 262176 | tf_op jit(solution)/shard_map/ppermute | solution.py:222
  223.7 0.4 fusion.59
  224.1 0.3 collective-permute-start.3
  224.4 15.1 %collective-permute-done.3 = bf16[4,4,32,1024]{3,2,1,0:T(8,128)(2,1)S(1)} collective-permute-done((bf16[4,4,32,1024]{3,2,1,0:T(8,128)(2,1)S(1)}, bf16[4,4,32,1024]{3,2,1,0:T(8,128)(2,1)S(1)}, u32[]{:S(2)}, u32[]{:S(2)}) %collective-permute-start.3) | collective-permute-done | bytes 1048608 | tf_op jit(solution)/shard_map/ppermute | solution.py:222
  239.5 0.4 fusion.49
  240.0 2.4 convert_reduce_fusion
  242.5 0.7 fusion.38
  243.2 25.5 %fusion.40 = bf16[1024,1024]{1,0:T(8,128)(2,1)} fusion(bf16[1024,1024]{1,0:T(8,128)(2,1)S(1)} %get-tuple-element.152, bf16[4096,1024]{1,0:T(8,128)(2,1)} %bitcast.85, bf16[4096,1024]{1,0:T(8,128)(2,1)} %bitcast.84, f32[1024]{0:T(1024)S(1)} %add_rsqrt_fusion.1, f32[1024]{0:T(1024)S(1)} %broadcast_multiply_fusion.1), kind=kOutput, calls=%fused_computation.41 | convolution fusion | flops 17224957952 | bytes 20979712 | tf_op jit(solution)/shard_map/dot_general | solution.py:366
  (39 shorter events, 1.4 us)
Async XLA Ops:
  0.0 130.4 %copy-start = (f32[225,16]{0,1:T(8,128)S(1)}, f32[225,16]{0,1:T(8,128)}, u32[]{:S(2)}) copy-start(f32[225,16]{0,1:T(8,128)} %param.14) | copy-start | bytes 43204
  0.0 4.4 %copy-start.2 = (bf16[4,8,32,1024]{3,2,1,0:T(8,128)(2,1)S(1)}, bf16[4,8,32,1024]{3,2,1,0:T(8,128)(2,1)}, u32[]{:S(2)}) copy-start(bf16[4,8,32,1024]{3,2,1,0:T(8,128)(2,1)} %param.9) | copy-start | bytes 6291460
  6.2 123.5 %copy-start.4 = (s32[64,128]{1,0:T(8,128)S(1)}, s32[64,128]{1,0:T(8,128)}, u32[]{:S(2)}) copy-start(s32[64,128]{1,0:T(8,128)} %param.15) | copy-start | bytes 98308
  6.2 128.1 %collective-permute-start = (bf16[4,4,32,1024]{3,2,1,0:T(8,128)(2,1)}, bf16[4,4,32,1024]{3,2,1,0:T(8,128)(2,1)S(1)}, u32[]{:S(2)}, u32[]{:S(2)}) collective-permute-start(bf16[4,4,32,1024]{3,2,1,0:T(8,128)(2,1)} %get-tuple-element.150), channel_id=1, source_target_pairs={{0,28},{4,0},{8,4},{12,8},{16,12},{20,16},{24,20},{28,24},{1,29},{... | collective-permute-start | bytes 3145736 | tf_op jit(solution)/shard_map/ppermute | solution.py:222
  134.3 9.0 %collective-permute-start.1 = (bf16[4,8,4,1024]{3,2,1,0:T(4,128)(2,1)S(1)}, bf16[4,8,4,1024]{3,2,1,0:T(4,128)(2,1)S(1)}, u32[]{:S(2)}, u32[]{:S(2)}) collective-permute-start(bf16[4,8,4,1024]{3,2,1,0:T(4,128)(2,1)S(1)} %pad_maximum_fusion.2), channel_id=1, source_target_pairs={{0,3},{1,0},{2,1},{3,2},{4,7},{5,4},{6,5},{7,6},{8,11},{9,8},{10,9... | collective-permute-start | bytes 786440 | tf_op jit(solution)/shard_map/ppermute | solution.py:222
  213.3 10.4 %collective-permute-start.2 = (bf16[4,8,4,1024]{3,2,1,0:T(4,128)(2,1)S(1)}, bf16[4,8,4,1024]{3,2,1,0:T(4,128)(2,1)S(1)}, u32[]{:S(2)}, u32[]{:S(2)}) collective-permute-start(bf16[4,8,4,1024]{3,2,1,0:T(4,128)(2,1)S(1)} %slice.46), channel_id=1, source_target_pairs={{0,1},{1,2},{2,3},{3,0},{4,5},{5,6},{6,7},{7,4},{8,9},{9,10},{10,1... | collective-permute-start | bytes 786440 | tf_op jit(solution)/shard_map/ppermute | solution.py:222
  223.7 16.3 %copy-start.3 = (bf16[4,8,32,1024]{3,2,1,0:T(8,128)(2,1)S(1)}, bf16[4,8,32,1024]{3,2,1,0:T(8,128)(2,1)}, u32[]{:S(2)}) copy-start(bf16[4,8,32,1024]{3,2,1,0:T(8,128)(2,1)} %param.9) | copy-start | bytes 6291460
  223.7 16.3 %copy-start.5 = (bf16[2,2,2,4,32,1024]{5,4,3,2,1,0:T(8,128)(2,1)S(1)}, bf16[2,2,2,4,32,1024]{5,4,3,2,1,0:T(8,128)(2,1)}, u32[]{:S(2)}) copy-start(bf16[2,2,2,4,32,1024]{5,4,3,2,1,0:T(8,128)(2,1)} %get-tuple-element.100) | copy-start | bytes 6291460
  224.1 15.4 %collective-permute-start.3 = (bf16[4,4,32,1024]{3,2,1,0:T(8,128)(2,1)S(1)}, bf16[4,4,32,1024]{3,2,1,0:T(8,128)(2,1)S(1)}, u32[]{:S(2)}, u32[]{:S(2)}) collective-permute-start(bf16[4,4,32,1024]{3,2,1,0:T(8,128)(2,1)S(1)} %fusion.59), channel_id=1, source_target_pairs={{0,4},{4,8},{8,12},{12,16},{16,20},{20,24},{24,28},{28,0},{1,5},{5... | collective-permute-start | bytes 3145736 | tf_op jit(solution)/shard_map/ppermute | solution.py:222
  243.2 25.5 %copy-start.1 = (f32[225,16]{0,1:T(8,128)S(1)}, f32[225,16]{0,1:T(8,128)}, u32[]{:S(2)}) copy-start(f32[225,16]{0,1:T(8,128)} %param.14) | copy-start | bytes 43204
